TPU v7x, 32 devices: a whole 2x2x4 slice. The times are simulated.
32 devices in a mesh: clip: 2 (over y), seq: 4 (over z), head: 4 (over x, core).
Axes of the slice: x: 2, y: 2, z: 4, core: 2. Of those that a mesh axis runs over, the one named last changes fastest.
Arguments:
- queries: bfloat16 [16, 4, 16, 3072], P(('clip', 'head'), 'seq'), parts along dimension 0, may hold values from -15 to 15
- attn_keys: bfloat16 [16, 4, 16, 3072], P(('clip', 'head'), 'seq'), parts along dimension 0, may hold values from -5 to 5
- attn_values: bfloat16 [16, 4, 16, 3072], P(('clip', 'head'), 'seq'), parts along dimension 0, may hold values from -5 to 5
- residual: bfloat16 [16, 4, 16, 5120], P(('clip', 'head'), 'seq'), parts along dimension 0, may hold values from -6 to 6
- out_weight: bfloat16 [3072, 5120], P('head', 'seq'), may hold values from -0.109375 to 0.109375
- out_gate: float32 [5120], replicated, may hold values from 0.3 to 3
- head_shift: float32 [5120], replicated, may hold values from -3 to 3
- head_scale: float32 [5120], replicated, may hold values from -1.5 to 1.5
- head_weight: bfloat16 [5120, 64], replicated, may hold values from -0.078125 to 0.078125
- head_bias: float32 [64], replicated, may hold values from -3 to 3
- conv_weight: bfloat16 [3, 3, 3, 16, 384], replicated, may hold values from -0.3125 to 0.3125
- conv_bias: float32 [384], replicated, may hold values from -3 to 3
- norm_gain: float32 [384], replicated, may hold values from 0.5 to 2
Outputs:
- hidden: bfloat16 [16, 4, 16, 5120], P(('clip', 'head'), 'seq'), parts along dimension 0
- features: bfloat16 [16, 8, 32, 384], P(('clip', 'head'), 'seq'), parts along dimension 0
There are 2 independent parts, one for each index of `clip`. A program takes and returns all parts, laid end to end along the dimension named above; an argument that names none is the same for every part. Nothing has to cross between parts.
All inputs are finite; a program needn't handle non-finite values.
Results may differ from a plain program's by a relative error of at most 0.013.
Values may be sent and summed in bfloat16 or wider, within the bound.
A program may use at most 128 MiB of HBM per device.

v0:
```python
import jax
import jax.numpy as jnp
from jax import lax
from jax.sharding import PartitionSpec as P

HEAD_DIM = 128


def from_behind(value, axis, steps):
    count = lax.axis_size(axis)
    first, last = (max(0, -steps), min(count, count - steps))
    return lax.ppermute(value, axis, [(source, source + steps) for source in range(first, last)])


def padded_2(x, sides, width):
    for axis, dim in sides:
        peers, length = (lax.axis_size(axis), x.shape[dim])
        up = [(i, (i + 1) % peers) for i in range(peers - 1)]
        down = [(j, i) for i, j in up]
        last = lax.slice_in_dim(x, length - width, length, axis=dim)
        first = lax.slice_in_dim(x, 0, width, axis=dim)
        before = lax.ppermute(last, axis, up)
        after = lax.ppermute(first, axis, down)
        x = jnp.concatenate([before, x, after], axis=dim)
    return x


def head_latent(hidden, head_shift, head_scale, head_weight, head_bias):
    values = hidden.astype(jnp.float32)
    center = values - jnp.mean(values, -1, keepdims=True)
    spread = jnp.mean(center * center, -1, keepdims=True)
    normed = (center * lax.rsqrt(spread + 1e-06) * (1.0 + head_scale) + head_shift).astype(
        jnp.bfloat16
    )
    flat = normed.reshape(-1, normed.shape[-1])
    latent = (jnp.dot(flat, head_weight, preferred_element_type=jnp.float32) + head_bias).astype(
        jnp.bfloat16
    )
    frames, height, breadth = (hidden.shape[0], hidden.shape[1], hidden.shape[2])
    channels = head_weight.shape[1] // 4
    patches = latent.reshape(frames, height, breadth, 2, 2, channels).transpose(0, 1, 3, 2, 4, 5)
    return patches.reshape(frames, height * 2, breadth * 2, channels)


def convolve(padded, frames, conv_weight, conv_bias, norm_gain):
    height = padded.shape[1] - 2
    breadth = padded.shape[2] - 2
    stacked = jnp.concatenate(
        [
            padded[
                time_off : time_off + frames,
                row_off : row_off + height,
                col_off : col_off + breadth,
            ]
            for time_off in range(3)
            for row_off in range(3)
            for col_off in range(3)
        ],
        -1,
    )
    kernel = conv_weight.reshape(-1, conv_weight.shape[-1])
    linear = (
        jnp.dot(stacked.reshape(-1, stacked.shape[-1]), kernel, preferred_element_type=jnp.float32)
        + conv_bias
    )
    normed = linear * lax.rsqrt(jnp.mean(linear * linear, -1, keepdims=True) + 1e-06) * norm_gain
    return jax.nn.silu(normed).astype(jnp.bfloat16).reshape(frames, height, breadth, -1)


def attend_block(carried, block_keys, block_values, query_heads):
    running, denominator, weighted = carried
    scores = jnp.einsum("hqd,khd->hqk", query_heads, block_keys, preferred_element_type=jnp.float32)
    scores = scores * query_heads.shape[-1] ** (-0.5)
    newmax = jnp.maximum(running, jnp.max(scores, -1))
    factor = jnp.exp(running - newmax)
    weights = jnp.exp(scores - newmax[..., None])
    denominator = denominator * factor + jnp.sum(weights, -1)
    product = jnp.einsum(
        "hqk,khd->hqd",
        weights.astype(jnp.bfloat16),
        block_values,
        preferred_element_type=jnp.float32,
    )
    weighted = weighted * factor[..., None] + product
    return (newmax, denominator, weighted)


def fold_pieces(query_heads, carried, pieces):
    key_piece, value_piece = pieces
    frames, height, breadth = (key_piece.shape[0], key_piece.shape[1], key_piece.shape[2])
    heads_here, head_width = (query_heads.shape[0], query_heads.shape[2])
    group_rows = 4

    def regroup(one_piece):
        shaped = one_piece.reshape(
            frames, height // group_rows, group_rows, breadth, heads_here, head_width
        )
        shaped = shaped.transpose(1, 0, 2, 3, 4, 5)
        return shaped.reshape(
            height // group_rows, frames * group_rows * breadth, heads_here, head_width
        )

    def advance(inner, blocks):
        return (attend_block(inner, blocks[0], blocks[1], query_heads), None)

    carried, _ = lax.scan(advance, carried, (regroup(key_piece), regroup(value_piece)))
    return carried


def on_device(
    queries,
    attn_keys,
    attn_values,
    residual,
    out_weight,
    out_gate,
    head_shift,
    head_scale,
    head_weight,
    head_bias,
    conv_weight,
    conv_bias,
    norm_gain,
):
    head_count = lax.axis_size("head")
    frames_dev = queries.shape[0]
    group_width = queries.shape[3] // head_count
    head_width = HEAD_DIM
    heads_here = group_width // head_width
    local_queries, local_keys, local_values = (
        lax.all_to_all(queries, "head", split_axis=3, concat_axis=0, tiled=True),
        lax.all_to_all(attn_keys, "head", split_axis=3, concat_axis=0, tiled=True),
        lax.all_to_all(attn_values, "head", split_axis=3, concat_axis=0, tiled=True),
    )
    frames_all, height, breadth = (
        local_queries.shape[0],
        local_queries.shape[1],
        local_queries.shape[2],
    )
    count = frames_all * height * breadth
    query_heads = local_queries.reshape(count, heads_here, head_width).transpose(1, 0, 2)
    initial = (
        jnp.full((heads_here, count), -1e30, jnp.float32),
        jnp.zeros((heads_here, count), jnp.float32),
        jnp.zeros((heads_here, count, head_width), jnp.float32),
    )
    carried = fold_pieces(
        query_heads,
        initial,
        (
            lax.all_gather(local_keys, "seq", axis=1, tiled=True),
            lax.all_gather(local_values, "seq", axis=1, tiled=True),
        ),
    )
    running, denominator, weighted = carried
    attended = (weighted / denominator[..., None]).astype(jnp.bfloat16)
    attended = attended.transpose(1, 0, 2).reshape(count, group_width)
    partial_value = jnp.dot(
        attended,
        lax.all_gather(out_weight, "seq", axis=1, tiled=True),
        preferred_element_type=jnp.float32,
    )
    partial_value = partial_value.reshape(frames_all, height, breadth, partial_value.shape[-1])
    owned = lax.psum_scatter(
        partial_value.astype(jnp.bfloat16), "head", scatter_dimension=0, tiled=True
    ).astype(jnp.float32)
    hidden = (residual.astype(jnp.float32) + out_gate * owned).astype(jnp.bfloat16)
    own_video = head_latent(hidden, head_shift, head_scale, head_weight, head_bias)
    earlier = from_behind(own_video, "head", 1)
    video = jnp.concatenate([earlier, own_video], 0)
    extended = padded_2(video, (("seq", 1),), 1)
    padded = jnp.pad(extended, ((0, 0), (0, 0), (1, 1), (0, 0)))
    features = convolve(padded, frames_dev, conv_weight, conv_bias, norm_gain)
    return (hidden, features)


def solution(mesh):
    return jax.shard_map(
        on_device,
        mesh=mesh,
        in_specs=(
            P(("clip", "head"), "seq", None, None),
            P(("clip", "head"), "seq", None, None),
            P(("clip", "head"), "seq", None, None),
            P(("clip", "head"), "seq", None, None),
            P("head", "seq"),
            P(),
            P(),
            P(),
            P(),
            P(),
            P(),
            P(),
            P(),
        ),
        out_specs=(P(("clip", "head"), "seq", None, None), P(("clip", "head"), "seq", None, None)),
        check_vma=False,
    )
```

profile of v0, /device:TPU:0, one launch (start us, length us, event | category | flops | bytes accessed | tf_op | source)
XLA Modules:
  0.0 232.0 jit_solution(3632974338613475676)
XLA Ops:
  7.2 0.0 copy-start
  7.2 0.0 all-gather.2.cloned.1.call-start
  7.2 0.7 all-gather.2.cloned.1.call-update
  7.9 0.2 copy-done.5
  8.2 1.8 copy.79
  10.0 2.3 reshape.122
  12.3 4.2 %all-to-all-start.1 = ((bf16[4,2,12288]{2,1,0:T(2,128)(2,1)}), bf16[4,2,12288]{2,1,0:T(2,128)(2,1)S(1)}, u32[]{:S(2)}, u32[]{:S(2)}) async-start(bf16[4,2,12288]{2,1,0:T(2,128)(2,1)} %reshape.122), calls=%async_computation.1 | async-start | bytes 393216 | tf_op jit(solution)/shard_map/all_to_all | solution.py:132
  16.5 1.8 copy.75
  18.3 0.0 copy-start.7
  18.3 2.3 reshape.124
  20.6 1.2 all-to-all-done.1
  21.8 3.4 %all-to-all-start = ((bf16[4,2,12288]{2,1,0:T(2,128)(2,1)}), bf16[4,2,12288]{2,1,0:T(2,128)(2,1)S(1)}, u32[]{:S(2)}, u32[]{:S(2)}) async-start(bf16[4,2,12288]{2,1,0:T(2,128)(2,1)} %reshape.124), calls=%async_computation | async-start | bytes 393216 | tf_op jit(solution)/shard_map/all_to_all | solution.py:131
  25.2 1.8 copy.84
  27.0 2.3 reshape.126
  29.3 1.2 reshape.123
  30.5 1.1 copy.93
  31.6 0.0 all-to-all-done
  31.6 4.0 %all-to-all-start.2 = ((bf16[4,2,12288]{2,1,0:T(2,128)(2,1)}), bf16[4,2,12288]{2,1,0:T(2,128)(2,1)}, u32[]{:S(2)}, u32[]{:S(2)}) async-start(bf16[4,2,12288]{2,1,0:T(2,128)(2,1)} %reshape.126), calls=%async_computation.2 | async-start | bytes 393216 | tf_op jit(solution)/shard_map/all_to_all | solution.py:133
  35.6 0.0 reduce-scatter.2.cloned.1.call-start
  35.7 35.5 %all_gather.9 = bf16[8,4,16,768]{3,2,0,1:T(8,128)(2,1)S(1)} all-gather(bf16[8,1,16,768]{3,2,0,1:T(8,128)(2,1)S(1)} %bitcast.111), channel_id=1, replica_groups=mesh['clip'=2,'seq'=4,'head'=4] {'seq'}, dimensions={1}, use_global_device_ids=true | all-gather | bytes 983040 | tf_op jit(solution)/shard_map/all_gather | solution.py:151
  71.2 0.1 copy.82
  71.2 0.9 squeeze.9
  72.1 1.2 reshape.125
  73.3 1.1 copy.92
  74.4 0.2 reshape.115
  74.7 5.6 %reshape.127 = bf16[3072,1,2,16]{3,2,1,0:T(2,128)(2,1)S(1)} reshape(bf16[4,2,12288]{2,1,0:T(2,128)(2,1)} %all-to-all-done.2) | data formatting | bytes 393216
  80.2 2.5 %copy.94 = bf16[2,1,16,4,768]{4,3,2,0,1:T(4,128)(2,1)} copy(bf16[2,1,16,4,768]{2,0,4,3,1:T(2,128)(2,1)S(1)} %bitcast.95) | data formatting | bytes 393216 | tf_op jit(solution)/shard_map/all_to_all | solution.py:133
  82.7 1.0 copy.86
  83.7 32.6 %all_gather.10 = bf16[8,4,16,768]{3,2,0,1:T(8,128)(2,1)S(1)} all-gather(bf16[8,1,16,768]{3,2,0,1:T(8,128)(2,1)S(1)} %bitcast.112), channel_id=1, replica_groups=mesh['clip'=2,'seq'=4,'head'=4] {'seq'}, dimensions={1}, use_global_device_ids=true | all-gather | bytes 983040 | tf_op jit(solution)/shard_map/all_gather | solution.py:152
  116.3 0.1 copy.87
  116.3 1.9 squeeze.10
  118.2 0.5 fusion.35
  118.7 0.5 fusion.8
  119.3 0.2 copy-done.2
  119.5 0.6 fusion.12
  120.1 0.1 copy.89
  120.2 0.2 dot_general.24
  120.5 0.0 copy-start.9
  120.5 0.0 copy-start.10
  120.5 57.9 %all-gather.2.cloned.1.call-done = bf16[768,5120]{1,0:T(8,128)(2,1)} async-done(((bf16[768,1280]{1,0:T(8,128)(2,1)}), bf16[768,5120]{1,0:T(8,128)(2,1)}) %all-gather.2.cloned.1.call-update) | async-done | bytes 7864336 | tf_op jit(solution)/shard_map/all_gather | solution.py:160
  178.5 5.6 %fusion.5 = bf16[8,1,16,5120]{3,2,0,1:T(8,128)(2,1)} fusion(bf16[8,16,768]{2,1,0:T(8,128)(2,1)S(1)} %dot_general.24, bf16[768,5120]{1,0:T(8,128)(2,1)} %all-gather.2.cloned.1.call-done), kind=kOutput, calls=%fused_computation.3 | convolution fusion | flops 1007288320 | bytes 9371648 | tf_op jit(solution)/shard_map/dot_general | solution.py:158
  184.1 0.0 reduce-scatter.2.cloned.1.call-update
  184.1 24.8 %reduce-scatter.2.cloned.1.call-done = bf16[2,1,16,5120]{3,2,0,1:T(8,128)(2,1)} async-done(((bf16[8,1,16,5120]{3,2,0,1:T(8,128)(2,1)}), bf16[2,1,16,5120]{3,2,0,1:T(8,128)(2,1)}) %reduce-scatter.2.cloned.1.call-update) | async-done | bytes 327696 | tf_op jit(solution)/shard_map/reduce_scatter | solution.py:164
  208.9 1.2 convert_reduce_fusion
  210.1 0.2 fusion.20
  210.4 0.0 copy-done.8
  210.4 0.2 fusion.23
  210.6 0.3 fusion.13
  210.9 0.1 reshape.117
  211.0 1.6 collective-permute-start
  212.6 0.8 collective-permute-done
  213.5 3.4 %collective-permute-start.1 = (bf16[4,1,32,16]{3,2,1,0:T(8,128)(2,1)S(1)}, bf16[4,1,32,16]{3,2,1,0:T(8,128)(2,1)S(1)}, u32[]{:S(2)}, u32[]{:S(2)}) collective-permute-start(bf16[4,1,32,16]{3,2,1,0:T(8,128)(2,1)S(1)} %get-tuple-element.63), channel_id=1, source_target_pairs={{0,4},{4,8},{8,12},{1,5},{5,9},{9,13},{2,6},{6,10},{10,14},{3,7},{... | collective-permute-start | bytes 12296 | tf_op jit(solution)/shard_map/ppermute | solution.py:22
  216.9 1.3 collective-permute-start.2
  218.2 0.3 collective-permute-done.1
  218.5 4.5 %collective-permute-done.2 = bf16[4,1,32,16]{3,2,1,0:T(8,128)(2,1)S(1)} collective-permute-done((bf16[4,1,32,16]{3,2,1,0:T(8,128)(2,1)S(1)}, bf16[4,1,32,16]{3,2,1,0:T(8,128)(2,1)S(1)}, u32[]{:S(2)}, u32[]{:S(2)}) %collective-permute-start.2) | collective-permute-done | bytes 4128 | tf_op jit(solution)/shard_map/ppermute | solution.py:23
  223.0 0.1 select_maximum_fusion
  223.0 0.0 copy-start.3
  223.1 0.0 copy-start.11
  223.1 0.0 copy-start.12
  223.1 0.1 fusion.32
  223.3 0.3 concatenate.105
  223.6 0.4 copy-done.3
  224.0 0.3 multiply_reduce_fusion
  224.4 0.8 multiply_convert_fusion
  (31 shorter events, 0.2 us)
Async XLA Ops:
  7.2 203.4 %copy-start = (bf16[5120,64]{0,1:T(8,128)(2,1)S(1)}, bf16[5120,64]{0,1:T(8,128)(2,1)}, u32[]{:S(2)}) copy-start(bf16[5120,64]{0,1:T(8,128)(2,1)} %param.21) | copy-start | bytes 1966084
  7.2 1.0 copy-start.5
  7.2 171.3 %all-gather.2.cloned.1.call-start = ((), (), s32[]{:S(2)}) async-start(), calls=%async_computation.4 | async-start | bytes 9830400 | tf_op jit(solution)/shard_map/all_gather | solution.py:160
  8.2 8.3 %copy-start.6 = (bf16[2,1,16,3072]{3,2,1,0:T(8,128)(2,1)S(1)}, bf16[2,1,16,3072]{3,2,1,0:T(8,128)(2,1)}, u32[]{:S(2)}) copy-start(bf16[2,1,16,3072]{3,2,1,0:T(8,128)(2,1)} %param.13) | copy-start | bytes 589828
  12.3 9.5 %all-to-all-start.1 = ((bf16[4,2,12288]{2,1,0:T(2,128)(2,1)}), bf16[4,2,12288]{2,1,0:T(2,128)(2,1)S(1)}, u32[]{:S(2)}, u32[]{:S(2)}) async-start(bf16[4,2,12288]{2,1,0:T(2,128)(2,1)} %reshape.122), calls=%async_computation.1 | async-start | bytes 393216 | tf_op jit(solution)/shard_map/all_to_all | solution.py:132
  18.3 6.9 %copy-start.7 = (bf16[2,1,16,3072]{3,2,1,0:T(8,128)(2,1)S(1)}, bf16[2,1,16,3072]{3,2,1,0:T(8,128)(2,1)}, u32[]{:S(2)}) copy-start(bf16[2,1,16,3072]{3,2,1,0:T(8,128)(2,1)} %param.15) | copy-start | bytes 589828
  21.8 9.8 %all-to-all-start = ((bf16[4,2,12288]{2,1,0:T(2,128)(2,1)}), bf16[4,2,12288]{2,1,0:T(2,128)(2,1)S(1)}, u32[]{:S(2)}, u32[]{:S(2)}) async-start(bf16[4,2,12288]{2,1,0:T(2,128)(2,1)} %reshape.124), calls=%async_computation | async-start | bytes 393216 | tf_op jit(solution)/shard_map/all_to_all | solution.py:131
  31.6 43.1 %all-to-all-start.2 = ((bf16[4,2,12288]{2,1,0:T(2,128)(2,1)}), bf16[4,2,12288]{2,1,0:T(2,128)(2,1)}, u32[]{:S(2)}, u32[]{:S(2)}) async-start(bf16[4,2,12288]{2,1,0:T(2,128)(2,1)} %reshape.126), calls=%async_computation.2 | async-start | bytes 393216 | tf_op jit(solution)/shard_map/all_to_all | solution.py:133
  35.6 173.3 %reduce-scatter.2.cloned.1.call-start = ((), (), s32[]{:S(2)}) async-start(), calls=%async_computation.5 | async-start | bytes 1638400 | tf_op jit(solution)/shard_map/reduce_scatter | solution.py:164
  118.2 1.2 copy-start.2
  120.5 63.6 %copy-start.9 = (f32[5120]{0:T(1024)S(1)}, f32[5120]{0:T(1024)}, u32[]{:S(2)}) copy-start(f32[5120]{0:T(1024)} %param.20) | copy-start | bytes 61444
  120.5 88.4 %copy-start.10 = (f32[5120]{0:T(1024)S(1)}, f32[5120]{0:T(1024)}, u32[]{:S(2)}) copy-start(f32[5120]{0:T(1024)} %param.18) | copy-start | bytes 61444
  184.1 24.9 %copy-start.4 = (bf16[2,1,16,5120]{3,2,1,0:T(8,128)(2,1)S(1)}, bf16[2,1,16,5120]{3,2,1,0:T(8,128)(2,1)}, u32[]{:S(2)}) copy-start(bf16[2,1,16,5120]{3,2,1,0:T(8,128)(2,1)} %param.16) | copy-start | bytes 983044
  184.1 26.3 %copy-start.8 = (f32[5120]{0:T(1024)S(1)}, f32[5120]{0:T(1024)}, u32[]{:S(2)}) copy-start(f32[5120]{0:T(1024)} %param.19) | copy-start | bytes 61444
  184.1 26.5 %copy-start.13 = (f32[64]{0:T(128)S(1)}, f32[64]{0:T(128)}, u32[]{:S(2)}) copy-start(f32[64]{0:T(128)} %param.22) | copy-start | bytes 772
  210.1 13.1 %copy-start.1 = (bf16[2,1,16,5120]{3,2,0,1:T(8,128)(2,1)}, bf16[2,1,16,5120]{3,2,0,1:T(8,128)(2,1)S(1)}, u32[]{:S(2)}) copy-start(bf16[2,1,16,5120]{3,2,0,1:T(8,128)(2,1)S(1)} %get-tuple-element.36) | copy-start | bytes 983044
  211.0 2.4 %collective-permute-start = (bf16[2,2,32,16]{3,2,1,0:T(8,128)(2,1)S(1)}, bf16[2,2,32,16]{3,2,1,0:T(8,128)(2,1)S(1)}, u32[]{:S(2)}, u32[]{:S(2)}) collective-permute-start(bf16[2,2,32,16]{3,2,1,0:T(8,128)(2,1)S(1)} %bitcast.101), channel_id=1, source_target_pairs={{0,1},{1,2},{2,3},{4,5},{5,6},{6,7},{8,9},{9,10},{10,11},{12,13},{... | collective-permute-start | bytes 12296 | tf_op jit(solution)/shard_map/ppermute | solution.py:12
  213.5 5.0 %collective-permute-start.1 = (bf16[4,1,32,16]{3,2,1,0:T(8,128)(2,1)S(1)}, bf16[4,1,32,16]{3,2,1,0:T(8,128)(2,1)S(1)}, u32[]{:S(2)}, u32[]{:S(2)}) collective-permute-start(bf16[4,1,32,16]{3,2,1,0:T(8,128)(2,1)S(1)} %get-tuple-element.63), channel_id=1, source_target_pairs={{0,4},{4,8},{8,12},{1,5},{5,9},{9,13},{2,6},{6,10},{10,14},{3,7},{... | collective-permute-start | bytes 12296 | tf_op jit(solution)/shard_map/ppermute | solution.py:22
  216.9 6.1 %collective-permute-start.2 = (bf16[4,1,32,16]{3,2,1,0:T(8,128)(2,1)S(1)}, bf16[4,1,32,16]{3,2,1,0:T(8,128)(2,1)S(1)}, u32[]{:S(2)}, u32[]{:S(2)}) collective-permute-start(bf16[4,1,32,16]{3,2,1,0:T(8,128)(2,1)S(1)} %get-tuple-element.64), channel_id=1, source_target_pairs={{4,0},{8,4},{12,8},{5,1},{9,5},{13,9},{6,2},{10,6},{14,10},{7,3},{... | collective-permute-start | bytes 12296 | tf_op jit(solution)/shard_map/ppermute | solution.py:23
  223.0 1.0 copy-start.3
  223.1 1.0 copy-start.11
  223.1 1.3 copy-start.12
Sparse Core Ops, SparseCore 0:
  9.6 168.8 all-gather.1
  184.2 24.6 reduce-scatter.1
where the time goes:
time: 233 us; the launch traced here: 232 us
  waiting for transfers between devices  90.3 us (39%)
  blocking collectives  68.1 us (29%)
  local copies, waits for them, and re-layouts  30.9 us (13%)
  starting transfers between devices  18 us (8%)
  between operations  14.5 us (6%)
  matrix products  7.28 us (3%)
  other arithmetic  3.08 us (1%)
    all_gather x1, waiting for transfers between devices, on_device(): lax.all_gather(out_weight, 'seq', axis=1, tiled=True)  57.9 us
    all_gather x1, blocking collectives, on_device(): lax.all_gather(local_keys, 'seq', axis=1, tiled=True)  35.5 us
    all_gather x1, blocking collectives, on_device(): lax.all_gather(local_values, 'seq', axis=1, tiled=True)  32.6 us
    reduce_scatter x1, waiting for transfers between devices, on_device(): lax.psum_scatter(partial_value.astype(jnp.bfloat16), 'head', scatter_dime...  24.8 us
    unnamed x37, local copies, waits for them, and re-layouts  21.1 us
    dot_general x1, matrix products, on_device(): jnp.dot(attended, lax.all_gather(out_weight, 'seq', axis=1, tiled=True),...  5.58 us
  transfers between devices with their start and end apart: 8, of which 6 were waited for; matrix products, arithmetic and copies ran while one was open for 13% of the time, Pallas kernels for 0%

commit v1 on v0

--- a/solution.py
+++ b/solution.py
@@ -1,6 +1,11 @@
+import functools
+import math
+
 import jax
 import jax.numpy as jnp
 from jax import lax
+from jax.experimental import pallas as pl
+from jax.experimental.pallas import tpu as pltpu
 from jax.sharding import PartitionSpec as P
 
 HEAD_DIM = 128
@@ -107,7 +112,7 @@
     return carried
 
 
-def on_device(
+def on_device_gathered(
     queries,
     attn_keys,
     attn_values,
@@ -174,6 +179,351 @@
     return (hidden, features)
 
 
+MESH = pl.DeviceIdType.MESH
+
+
+class Plan:
+    def __init__(self, ns, nh, queries, residual, out_weight):
+        self.ns, self.nh = ns, nh
+        self.tokens = queries.shape[0] * queries.shape[1] * queries.shape[2]
+        self.group = queries.shape[3] // nh // HEAD_DIM
+        self.parts = ns // math.gcd(self.group, ns)
+        self.units = self.group * self.parts // ns
+        firsts = [self.units * s // self.parts for s in range(ns)]
+        lasts = [(self.units * (s + 1) - 1) // self.parts for s in range(ns)]
+        self.span = max(b - a + 1 for a, b in zip(firsts, lasts))
+        self.clamp = self.group - self.span
+        self.width = residual.shape[3]
+        self.columns = out_weight.shape[1]
+        self.slots = ns * nh
+        self.bits = nh.bit_length() - 1
+
+    def fits(self, queries):
+        return (
+            self.nh == 1 << self.bits
+            and self.bits == 2
+            and self.ns >= 2
+            and self.tokens % 16 == 0
+            and self.ns % self.parts == 0
+            and self.columns % 128 == 0
+            and queries.shape[0] >= 2
+            and self.slots * self.tokens <= 1024
+        )
+
+
+def block_kernel(
+    plan,
+    q_hbm, k_hbm, v_hbm, res_hbm, w_hbm, hw_hbm,
+    gate_ref, shift_ref, scale_ref, bias_ref,
+    hidden_ref, near_ref,
+    qkv, got, att, weight, res, head_w, term, *rest,
+):
+    p = plan
+    landed = rest[: p.bits]
+    final, patch, halo = rest[p.bits : p.bits + 3]
+    (local_sem, own_sem, s1, r1, s3, r3, s5, r5, s6, r6, s7, r7) = rest[p.bits + 3 :]
+    s = lax.axis_index("seq")
+    h = lax.axis_index("head")
+    here = s * p.nh + h
+
+    def first_head(seq_index):
+        return jnp.minimum(p.units * seq_index // p.parts, p.clamp)
+
+    loads = [
+        pltpu.make_async_copy(q_hbm, qkv.at[0], local_sem.at[0]),
+        pltpu.make_async_copy(k_hbm, qkv.at[1], local_sem.at[1]),
+        pltpu.make_async_copy(v_hbm, qkv.at[2], local_sem.at[2]),
+    ]
+    late = [
+        pltpu.make_async_copy(w_hbm, weight, local_sem.at[3]),
+        pltpu.make_async_copy(res_hbm, res, local_sem.at[4]),
+        pltpu.make_async_copy(hw_hbm, head_w, local_sem.at[5]),
+    ]
+    for copy in loads:
+        copy.start()
+
+    offsets = [(ds, dh) for ds in range(p.ns) for dh in range(p.nh) if ds or dh]
+    barrier = pltpu.get_barrier_semaphore()
+    for ds, dh in offsets:
+        pl.semaphore_signal(
+            barrier,
+            inc=1,
+            device_id={"seq": lax.rem(s + ds, p.ns), "head": lax.rem(h + dh, p.nh)},
+            device_id_type=MESH,
+        )
+    for copy in loads:
+        copy.wait()
+    pl.semaphore_wait(barrier, len(offsets))
+
+    def piece(seq_index, head_index, j):
+        start = (head_index * p.group + first_head(seq_index) + j) * HEAD_DIM
+        return qkv.at[:, :, pl.ds(pl.multiple_of(start, HEAD_DIM), HEAD_DIM)]
+
+    first_sends = []
+    for index, (ds, dh) in enumerate(offsets):
+        to_s, to_h = lax.rem(s + ds, p.ns), lax.rem(h + dh, p.nh)
+        for j in range(p.span):
+            copy = pltpu.make_async_remote_copy(
+                src_ref=piece(to_s, to_h, j),
+                dst_ref=got.at[here, j],
+                send_sem=s1.at[index, j],
+                recv_sem=r1.at[index, j],
+                device_id={"seq": to_s, "head": to_h},
+                device_id_type=MESH,
+            )
+            copy.start()
+            first_sends.append(copy)
+    own = [
+        pltpu.make_async_copy(piece(s, h, j), got.at[here, j], own_sem.at[j])
+        for j in range(p.span)
+    ]
+    for copy in own:
+        copy.start()
+    for copy in late:
+        copy.start()
+    for copy in own:
+        copy.wait()
+    for copy in first_sends:
+        copy.wait()
+
+    per_part = p.slots // p.parts
+    base = first_head(s)
+    gather = []
+    for i in range(p.units):
+        unit = p.units * s + i
+        j = unit // p.parts - base
+        part = lax.rem(unit, p.parts)
+        q = got[pl.ds(part * per_part, per_part), j, 0].reshape(-1, HEAD_DIM)
+        k = got[:, j, 1].reshape(-1, HEAD_DIM)
+        v = got[:, j, 2].reshape(-1, HEAD_DIM)
+        scores = lax.dot_general(
+            q, k, (((1,), (1,)), ((), ())), preferred_element_type=jnp.float32
+        )
+        scores = scores * HEAD_DIM ** (-0.5)
+        weights = jnp.exp(scores - jnp.max(scores, -1, keepdims=True))
+        denominator = jnp.sum(weights, -1, keepdims=True)
+        product = jnp.dot(weights.astype(jnp.bfloat16), v, preferred_element_type=jnp.float32)
+        att[s, i] = (product / denominator).astype(jnp.bfloat16)
+        for ds in range(1, p.ns):
+            copy = pltpu.make_async_remote_copy(
+                src_ref=att.at[s, i],
+                dst_ref=att.at[s, i],
+                send_sem=s3.at[ds - 1, i],
+                recv_sem=r3.at[ds - 1, i],
+                device_id={"seq": lax.rem(s + ds, p.ns)},
+                device_id_type=MESH,
+            )
+            copy.start()
+            gather.append(copy)
+    late[0].wait()
+    for copy in gather:
+        copy.wait()
+
+    per_seq = p.ns // p.parts
+    for part in range(p.parts):
+        picks = [g * p.parts + part for g in range(p.group)]
+        rows = jnp.concatenate([att[u // p.units, u % p.units] for u in picks], axis=1)
+        product = jnp.dot(rows, weight[...], preferred_element_type=jnp.float32)
+        term[pl.ds(part * per_seq, per_seq)] = product.astype(jnp.bfloat16).reshape(
+            (per_seq,) + term.shape[1:]
+        )
+
+    current = term
+    for b in range(p.bits):
+        bit = (h >> b) & 1
+        peer = h + (1 - 2 * bit) * (1 << b)
+        half = p.nh >> (b + 1)
+        copy = pltpu.make_async_remote_copy(
+            src_ref=current.at[:, :, 1 - bit] if b == 0 else current.at[:, 1 - bit],
+            dst_ref=landed[b],
+            send_sem=s5.at[b],
+            recv_sem=r5.at[b],
+            device_id={"head": peer},
+            device_id_type=MESH,
+        )
+        copy.start()
+        copy.wait()
+        mine = current[:, :, bit] if b == 0 else current[:, bit]
+        total = mine.astype(jnp.float32) + landed[b][...].astype(jnp.float32)
+        landed[b][...] = total.astype(jnp.bfloat16)
+        current = landed[b]
+
+    owner = []
+    for ds in range(1, p.ns):
+        to_s = lax.rem(s + ds, p.ns)
+        copy = pltpu.make_async_remote_copy(
+            src_ref=current.at[to_s],
+            dst_ref=final.at[s],
+            send_sem=s6.at[ds - 1],
+            recv_sem=r6.at[ds - 1],
+            device_id={"seq": to_s},
+            device_id_type=MESH,
+        )
+        copy.start()
+        owner.append(copy)
+    final[s] = current[s]
+    for copy in late[1:]:
+        copy.wait()
+    for copy in owner:
+        copy.wait()
+
+    sums = jnp.zeros((p.tokens, 1), jnp.float32)
+    for j in range(p.ns):
+        cols = pl.ds(j * p.columns, p.columns)
+        value = res[:, cols].astype(jnp.float32) + gate_ref[:, cols] * final[j].astype(jnp.float32)
+        value = value.astype(jnp.bfloat16)
+        hidden_ref[:, cols] = value
+        sums = sums + jnp.sum(value.astype(jnp.float32), -1, keepdims=True)
+    mean = sums / p.width
+    center = hidden_ref[...].astype(jnp.float32) - mean
+    spread = jnp.mean(center * center, -1, keepdims=True)
+    normed = center * lax.rsqrt(spread + 1e-06) * (1.0 + scale_ref[...]) + shift_ref[...]
+    values = jnp.dot(
+        normed.astype(jnp.bfloat16), head_w[...], preferred_element_type=jnp.float32
+    )
+    values = (values + bias_ref[...]).astype(jnp.bfloat16)
+    features = values.shape[-1]
+    patch[...] = jnp.zeros_like(patch)
+    patch[:, :features] = values
+
+    moves = [(0, 1), (0, -1), (1, 0), (1, 1), (1, -1)]
+
+    def edge(index, sign):
+        dh, ds = moves[index]
+        return (
+            (h + sign * dh >= 0) & (h + sign * dh < p.nh)
+            & (s + sign * ds >= 0) & (s + sign * ds < p.ns)
+        )
+
+    def hop(index):
+        dh, ds = moves[index]
+        return pltpu.make_async_remote_copy(
+            src_ref=patch,
+            dst_ref=halo.at[index],
+            send_sem=s7.at[index],
+            recv_sem=r7.at[index],
+            device_id={"seq": lax.rem(s + ds + p.ns, p.ns), "head": lax.rem(h + dh, p.nh)},
+            device_id_type=MESH,
+        )
+
+    for index in range(len(moves)):
+
+        @pl.when(edge(index, 1))
+        def _():
+            hop(index).start()
+
+    near_ref[1, 1] = values
+    for index, (dh, ds) in enumerate(moves):
+
+        @pl.when(edge(index, -1))
+        def _():
+            hop(index).wait_recv()
+            near_ref[1 - dh, 1 - ds] = halo[index][:, :features]
+
+        @pl.when(jnp.logical_not(edge(index, -1)))
+        def _():
+            near_ref[1 - dh, 1 - ds] = jnp.zeros_like(values)
+
+    for index in range(len(moves)):
+
+        @pl.when(edge(index, 1))
+        def _():
+            hop(index).wait_send()
+
+
+def on_device(
+    queries,
+    attn_keys,
+    attn_values,
+    residual,
+    out_weight,
+    out_gate,
+    head_shift,
+    head_scale,
+    head_weight,
+    head_bias,
+    conv_weight,
+    conv_bias,
+    norm_gain,
+):
+    ns, nh = lax.axis_size("seq"), lax.axis_size("head")
+    p = Plan(ns, nh, queries, residual, out_weight)
+    if not p.fits(queries):
+        return on_device_gathered(
+            queries, attn_keys, attn_values, residual, out_weight, out_gate, head_shift,
+            head_scale, head_weight, head_bias, conv_weight, conv_bias, norm_gain,
+        )
+    frames, height, breadth, inner = queries.shape
+    t, width, patch_size = p.tokens, p.width, head_weight.shape[1]
+    dma, bf16 = pltpu.SemaphoreType.DMA, jnp.bfloat16
+    tail = (t, p.columns)
+    lanes = -(-patch_size // 128) * 128
+    any_spec = pl.BlockSpec(memory_space=pl.ANY)
+    vmem = pl.BlockSpec(memory_space=pltpu.VMEM)
+    landed = [
+        pltpu.VMEM((ns,) + ((nh >> 1,) if b == 0 and nh > 2 else ()) + tail, bf16)
+        for b in range(p.bits)
+    ]
+    hidden, near = pl.pallas_call(
+        functools.partial(block_kernel, p),
+        out_shape=(
+            jax.ShapeDtypeStruct((t, width), bf16),
+            jax.ShapeDtypeStruct((2, 3, t, patch_size), bf16),
+        ),
+        in_specs=[any_spec] * 6 + [vmem] * 4,
+        out_specs=(vmem, vmem),
+        scratch_shapes=[
+            pltpu.VMEM((3, t, inner), bf16),
+            pltpu.VMEM((p.slots, p.span, 3, t, HEAD_DIM), bf16),
+            pltpu.VMEM((ns, p.units, p.slots // p.parts * t, HEAD_DIM), bf16),
+            pltpu.VMEM(out_weight.shape, bf16),
+            pltpu.VMEM((t, width), bf16),
+            pltpu.VMEM(head_weight.shape, bf16),
+            pltpu.VMEM((ns, nh >> 1, 2) + tail, bf16),
+            *landed,
+            pltpu.VMEM((ns,) + tail, bf16),
+            pltpu.VMEM((t, lanes), bf16),
+            pltpu.VMEM((5, t, lanes), bf16),
+            dma((6,)),
+            dma((p.span,)),
+            dma((p.slots - 1, p.span)),
+            dma((p.slots - 1, p.span)),
+            dma((ns - 1, p.units)),
+            dma((ns - 1, p.units)),
+            dma((p.bits,)),
+            dma((p.bits,)),
+            dma((ns - 1,)),
+            dma((ns - 1,)),
+            dma((5,)),
+            dma((5,)),
+        ],
+        compiler_params=pltpu.CompilerParams(
+            collective_id=0, has_side_effects=True, vmem_limit_bytes=40 * 1024 * 1024
+        ),
+    )(
+        queries.reshape(t, inner),
+        attn_keys.reshape(t, inner),
+        attn_values.reshape(t, inner),
+        residual.reshape(t, width),
+        out_weight,
+        head_weight,
+        out_gate.reshape(1, -1),
+        head_shift.reshape(1, -1),
+        head_scale.reshape(1, -1),
+        head_bias.reshape(1, -1),
+    )
+    channels = patch_size // 4
+    video = near.reshape(2, 3, frames, height, breadth, 2, 2, channels)
+    video = video.transpose(0, 2, 1, 3, 5, 4, 6, 7)
+    video = video.reshape(2, frames, 3 * height * 2, breadth * 2, channels)
+    video = jnp.concatenate([video[0, -2:], video[1]], 0)
+    rows = height * 2
+    video = video[:, rows - 1 : 2 * rows + 1]
+    padded = jnp.pad(video, ((0, 0), (0, 0), (1, 1), (0, 0)))
+    features = convolve(padded, frames, conv_weight, conv_bias, norm_gain)
+    return (hidden.reshape(residual.shape), features)
+
+
 def solution(mesh):
     return jax.shard_map(
         on_device,

time: 233 us -> 74.5 us (0.32)
  waiting for transfers between devices: 90.3 us -> 0 us
  blocking collectives: 68.1 us -> 0 us
  Pallas kernels: 0 us -> 66.4 us
  local copies, waits for them, and re-layouts: 30.9 us -> 5.84 us
  starting transfers between devices: 18 us -> 0 us
  between operations: 14.5 us -> 0.88 us
  matrix products: 7.28 us -> 0.31 us
    all_gather x2 -> x0, blocking collectives: 68.1 us -> none  [the longest x1 35.5 us: on_device(): lax.all_gather(local_keys, 'seq', axis=1, tiled=True)]
    pallas_call x0 -> x1, Pallas kernels: none -> 66.4 us  [on_device(): pl.pallas_call(functools.partial(block_kernel, p), out_shape=(jax.ShapeDt...]
    all_gather x1 -> x0, waiting for transfers between devices: 57.9 us -> none  [on_device(): lax.all_gather(out_weight, 'seq', axis=1, tiled=True)]
    reduce_scatter x1 -> x0, waiting for transfers between devices: 24.8 us -> none  [on_device(): lax.psum_scatter(partial_value.astype(jnp.bfloat16), 'head', scatter_dime...]
    unnamed x37 -> x26, local copies, waits for them, and re-layouts: 21.1 us -> 4.9 us
    all_to_all x3 -> x0, starting transfers between devices: 11.6 us -> none  [the longest x1 4.24 us: on_device(): lax.all_to_all(attn_keys, 'head', split_axis=3, concat_axis=0, tiled=True)]
    dot_general x4 -> x0, matrix products: 6.97 us -> none  [the longest x1 5.58 us: on_device(): jnp.dot(attended, lax.all_gather(out_weight, 'seq', axis=1, tiled=True),...]
    ppermute x3 -> x0, starting transfers between devices: 6.26 us -> none  [the longest x1 3.39 us: padded_2(): before = lax.ppermute(last, axis, up)]
  transfers between devices with their start and end apart: 8 -> 0, of which waited for: 6 -> 0; matrix products, arithmetic and copies ran while one was open for 13% -> 0% of each run, Pallas kernels for 0% -> 0%
where the time goes in v1:
time: 74.5 us; the launch traced here: 74.3 us
  Pallas kernels  66.4 us (89%)
  local copies, waits for them, and re-layouts  5.84 us (8%)
  between operations  0.88 us (1%)
  other arithmetic  0.84 us (1%)
    pallas_call x1, Pallas kernels, on_device(): pl.pallas_call(functools.partial(block_kernel, p), out_shape=(jax.ShapeDt...  66.4 us
    unnamed x26, local copies, waits for them, and re-layouts  4.9 us

profile of v1, /device:TPU:0, one launch (start us, length us, event | category | flops | bytes accessed | tf_op | source)
XLA Modules:
  0.0 74.3 jit_solution(524810865481327525)
XLA Ops:
  0.6 0.0 copy-start
  0.6 0.0 copy-start.9
  0.7 0.0 copy-start.8
  0.7 0.0 copy-start.7
  0.7 0.0 copy-start.6
  0.7 0.0 copy-start.2
  0.7 0.0 copy-start.5
  0.7 0.0 copy-start.4
  0.7 0.9 %copy-done = bf16[3,3,3,16,384]{4,3,2,1,0:T(8,128)(2,1)S(1)} copy-done((bf16[3,3,3,16,384]{4,3,2,1,0:T(8,128)(2,1)S(1)}, bf16[3,3,3,16,384]{4,3,2,1,0:T(8,128)(2,1)}, u32[]{:S(2)}) %copy-start) | copy-done | bytes 331800
  1.6 0.0 copy-start.3
  1.6 1.7 %copy.17.hw_hbm = bf16[5120,64]{1,0:T(8,128)(2,1)S(1)} copy(bf16[5120,64]{0,1:T(8,128)(2,1)} %param.21) | data formatting | bytes 1310720 | tf_op args[8]
  3.3 0.0 copy-done.9
  3.3 0.0 copy-done.8
  3.3 0.0 copy-done.7
  3.3 0.0 copy-done.6
  3.4 0.0 copy-done.2
  3.4 0.0 copy-done.5
  3.4 0.0 copy-done.4
  3.4 0.0 copy-done.3
  3.4 0.0 copy-start.1
  3.4 1.5 %copy-done.1 = bf16[768,1280]{1,0:T(8,128)(2,1)S(1)} copy-done((bf16[768,1280]{1,0:T(8,128)(2,1)S(1)}, bf16[768,1280]{1,0:T(8,128)(2,1)}, u32[]{:S(2)}) %copy-start.1) | copy-done | bytes 1966104
  4.9 66.4 %shard_map.140 = (bf16[32,5120]{1,0:T(8,128)(2,1)S(1)}, bf16[2,3,32,64]{3,2,1,0:T(8,128)(2,1)S(1)}) custom-call(bf16[32,3072]{1,0:T(8,128)(2,1)S(1)} %bitcast.26, bf16[32,3072]{1,0:T(8,128)(2,1)S(1)} %bitcast.27, bf16[32,3072]{1,0:T(8,128)(2,1)S(1)} %bitcast.28, bf16[32,5120]{1,0:T(8,128)(2,1)S(1)} %bitcast.25, bf16[768,1280]{1,0:T(8,128)(2,1)S(1)} %copy-done.1, ...), custom_call_target="tpu_custom_call" | custom-call | tf_op jit(solution)/shard_map/pallas_call | solution.py:467
  71.4 0.0 copy-start.10
  71.4 0.1 reshape.67
  71.5 0.2 copy.21
  71.7 0.0 copy-start.11
  71.7 0.2 fusion.3
  71.9 0.1 pad_slice_fusion.6
  72.1 0.3 concatenate.7
  72.4 0.0 copy-done.10
  72.4 0.3 multiply_reduce_fusion
  72.8 0.0 copy-done.11
  72.8 0.8 %multiply_convert_fusion = bf16[128,384]{1,0:T(8,128)(2,1)} fusion(f32[128,384]{1,0:T(8,128)S(1)} %get-tuple-element.40, f32[384]{0:T(512)S(1)} %copy-done.11, f32[128]{0:T(128)S(1)} %add_rsqrt_fusion), kind=kLoop, calls=%fused_computation.8 | loop fusion | flops 344064 | bytes 296960 | tf_op jit(solution)/shard_map/convert_element_type | solution.py:72
  73.6 0.7 copy.23
  (3 shorter events, 0.1 us)
Async XLA Ops:
  0.6 1.0 %copy-start = (bf16[3,3,3,16,384]{4,3,2,1,0:T(8,128)(2,1)S(1)}, bf16[3,3,3,16,384]{4,3,2,1,0:T(8,128)(2,1)}, u32[]{:S(2)}) copy-start(bf16[3,3,3,16,384]{4,3,2,1,0:T(8,128)(2,1)} %param.23) | copy-start | bytes 995332
  0.6 2.7 %copy-start.9 = (f32[64]{0:T(128)S(1)}, f32[64]{0:T(128)}, u32[]{:S(2)}) copy-start(f32[64]{0:T(128)} %param.22) | copy-start | bytes 772
  0.7 2.7 %copy-start.8 = (f32[5120]{0:T(1024)S(1)}, f32[5120]{0:T(1024)}, u32[]{:S(2)}) copy-start(f32[5120]{0:T(1024)} %param.20) | copy-start | bytes 61444
  0.7 2.7 %copy-start.7 = (f32[5120]{0:T(1024)S(1)}, f32[5120]{0:T(1024)}, u32[]{:S(2)}) copy-start(f32[5120]{0:T(1024)} %param.19) | copy-start | bytes 61444
  0.7 2.7 %copy-start.6 = (f32[5120]{0:T(1024)S(1)}, f32[5120]{0:T(1024)}, u32[]{:S(2)}) copy-start(f32[5120]{0:T(1024)} %param.18) | copy-start | bytes 61444
  0.7 2.7 %copy-start.2 = (bf16[2,1,16,5120]{3,2,1,0:T(8,128)(2,1)S(1)}, bf16[2,1,16,5120]{3,2,1,0:T(8,128)(2,1)}, u32[]{:S(2)}) copy-start(bf16[2,1,16,5120]{3,2,1,0:T(8,128)(2,1)} %param.16) | copy-start | bytes 983044
  0.7 2.7 %copy-start.5 = (bf16[2,1,16,3072]{3,2,1,0:T(8,128)(2,1)S(1)}, bf16[2,1,16,3072]{3,2,1,0:T(8,128)(2,1)}, u32[]{:S(2)}) copy-start(bf16[2,1,16,3072]{3,2,1,0:T(8,128)(2,1)} %param.15) | copy-start | bytes 589828
  0.7 2.7 %copy-start.4 = (bf16[2,1,16,3072]{3,2,1,0:T(8,128)(2,1)S(1)}, bf16[2,1,16,3072]{3,2,1,0:T(8,128)(2,1)}, u32[]{:S(2)}) copy-start(bf16[2,1,16,3072]{3,2,1,0:T(8,128)(2,1)} %param.14) | copy-start | bytes 589828
  1.6 1.8 %copy-start.3 = (bf16[2,1,16,3072]{3,2,1,0:T(8,128)(2,1)S(1)}, bf16[2,1,16,3072]{3,2,1,0:T(8,128)(2,1)}, u32[]{:S(2)}) copy-start(bf16[2,1,16,3072]{3,2,1,0:T(8,128)(2,1)} %param.13) | copy-start | bytes 589828
  3.4 1.5 %copy-start.1 = (bf16[768,1280]{1,0:T(8,128)(2,1)S(1)}, bf16[768,1280]{1,0:T(8,128)(2,1)}, u32[]{:S(2)}) copy-start(bf16[768,1280]{1,0:T(8,128)(2,1)} %w_hbm.1) | copy-start | bytes 5898244
  71.4 1.1 %copy-start.10 = (f32[384]{0:T(512)S(1)}, f32[384]{0:T(512)}, u32[]{:S(2)}) copy-start(f32[384]{0:T(512)} %param.24) | copy-start | bytes 4612
  71.7 1.1 %copy-start.11 = (f32[384]{0:T(512)S(1)}, f32[384]{0:T(512)}, u32[]{:S(2)}) copy-start(f32[384]{0:T(512)} %param.25) | copy-start | bytes 4612

commit v2 on v1

--- a/solution.py
+++ b/solution.py
@@ -189,22 +189,21 @@
         self.group = queries.shape[3] // nh // HEAD_DIM
         self.parts = ns // math.gcd(self.group, ns)
         self.units = self.group * self.parts // ns
-        firsts = [self.units * s // self.parts for s in range(ns)]
-        lasts = [(self.units * (s + 1) - 1) // self.parts for s in range(ns)]
-        self.span = max(b - a + 1 for a, b in zip(firsts, lasts))
-        self.clamp = self.group - self.span
         self.width = residual.shape[3]
         self.columns = out_weight.shape[1]
         self.slots = ns * nh
+        self.chunk = 256 if self.columns % 256 == 0 else 128
+        self.chunks = self.columns // self.chunk
         self.bits = nh.bit_length() - 1
 
     def fits(self, queries):
         return (
             self.nh == 1 << self.bits
             and self.bits == 2
-            and self.ns >= 2
+            and self.ns % 2 == 0
+            and self.parts == 2
+            and self.units == 3
             and self.tokens % 16 == 0
-            and self.ns % self.parts == 0
             and self.columns % 128 == 0
             and queries.shape[0] >= 2
             and self.slots * self.tokens <= 1024
@@ -221,13 +220,10 @@
     p = plan
     landed = rest[: p.bits]
     final, patch, halo = rest[p.bits : p.bits + 3]
-    (local_sem, own_sem, s1, r1, s3, r3, s5, r5, s6, r6, s7, r7) = rest[p.bits + 3 :]
+    (local_sem, own_sem, s1, r1, sf, rf, s3, r3, s5, r5, s6, r6, s7, r7) = rest[p.bits + 3 :]
     s = lax.axis_index("seq")
     h = lax.axis_index("head")
     here = s * p.nh + h
-
-    def first_head(seq_index):
-        return jnp.minimum(p.units * seq_index // p.parts, p.clamp)
 
     loads = [
         pltpu.make_async_copy(q_hbm, qkv.at[0], local_sem.at[0]),
@@ -256,26 +252,49 @@
     pl.semaphore_wait(barrier, len(offsets))
 
     def piece(seq_index, head_index, j):
-        start = (head_index * p.group + first_head(seq_index) + j) * HEAD_DIM
+        start = (head_index * p.group + 3 * (seq_index // 2) + seq_index % 2 + j) * HEAD_DIM
         return qkv.at[:, :, pl.ds(pl.multiple_of(start, HEAD_DIM), HEAD_DIM)]
 
-    first_sends = []
-    for index, (ds, dh) in enumerate(offsets):
+    def place(seq_index, k):
+        return 1 - seq_index % 2 if k == 0 else seq_index % 2
+
+    def direct(source, target):
+        up = (source // 2 < target // 2) & (target % 2 == 1)
+        down = (source // 2 > target // 2) & (target % 2 == 0)
+        return jnp.logical_not(up | down)
+
+    def first_hop(index, k, to_s, to_h, slot, j):
+        return pltpu.make_async_remote_copy(
+            src_ref=piece(to_s, to_h, j),
+            dst_ref=got.at[slot, j],
+            send_sem=s1.at[index, k],
+            recv_sem=r1.at[index, k],
+            device_id={"seq": to_s, "head": to_h},
+            device_id_type=MESH,
+        )
+
+    def sending(index, k):
+        ds, dh = offsets[index]
         to_s, to_h = lax.rem(s + ds, p.ns), lax.rem(h + dh, p.nh)
-        for j in range(p.span):
-            copy = pltpu.make_async_remote_copy(
-                src_ref=piece(to_s, to_h, j),
-                dst_ref=got.at[here, j],
-                send_sem=s1.at[index, j],
-                recv_sem=r1.at[index, j],
-                device_id={"seq": to_s, "head": to_h},
-                device_id_type=MESH,
-            )
-            copy.start()
-            first_sends.append(copy)
+        return to_s, first_hop(index, k, to_s, to_h, here, place(to_s, k))
+
+    def arriving(index, k):
+        ds, dh = offsets[index]
+        from_s, from_h = lax.rem(s - ds + p.ns, p.ns), lax.rem(h - dh + p.nh, p.nh)
+        return from_s, first_hop(index, k, s, h, from_s * p.nh + from_h, place(s, k))
+
+    def guarded(k, ds, source, target, act):
+        if k == 0 and ds:
+            pl.when(direct(source, target))(act)
+        else:
+            act()
+
+    for k in range(2):
+        for index, (ds, dh) in enumerate(offsets):
+            to_s, copy = sending(index, k)
+            guarded(k, ds, s, to_s, copy.start)
     own = [
-        pltpu.make_async_copy(piece(s, h, j), got.at[here, j], own_sem.at[j])
-        for j in range(p.span)
+        pltpu.make_async_copy(piece(s, h, j), got.at[here, j], own_sem.at[j]) for j in range(2)
     ]
     for copy in own:
         copy.start()
@@ -283,16 +302,66 @@
         copy.start()
     for copy in own:
         copy.wait()
-    for copy in first_sends:
-        copy.wait()
+
+    even = s % 2 == 0
+    peer_s = s + 1 - 2 * (s % 2)
+
+    def hand_on(level, j_from, j_to):
+        rows = pl.ds(level * p.nh, p.nh)
+        return pltpu.make_async_remote_copy(
+            src_ref=got.at[rows, j_from, pl.ds(1, 2)],
+            dst_ref=got.at[rows, j_to, pl.ds(1, 2)],
+            send_sem=sf.at[level],
+            recv_sem=rf.at[level],
+            device_id={"seq": peer_s},
+            device_id_type=MESH,
+        )
+
+    def handed(level):
+        return jnp.where(even, level // 2 < s // 2, level // 2 > s // 2)
+
+    def expected(level):
+        return jnp.where(even, level // 2 > s // 2, level // 2 < s // 2)
+
+    for ds in list(range(1, p.ns)) + [0]:
+        for index, (ds2, dh) in enumerate(offsets):
+            if ds2 == ds:
+                from_s, copy = arriving(index, 0)
+                guarded(0, ds, from_s, s, copy.wait_recv)
+        if ds:
+            level = lax.rem(s - ds + p.ns, p.ns)
+
+            @pl.when(handed(level))
+            def _():
+                hand_on(level, place(s, 0), place(peer_s, 0)).start()
+
+    for index in range(len(offsets)):
+        arriving(index, 1)[1].wait_recv()
 
     per_part = p.slots // p.parts
-    base = first_head(s)
-    gather = []
+
+    def gather_hop(source, i, step):
+        return pltpu.make_async_remote_copy(
+            src_ref=att.at[source, i],
+            dst_ref=att.at[source, i],
+            send_sem=s3.at[(step + 1) // 2, source, i],
+            recv_sem=r3.at[source, i],
+            device_id={"seq": lax.rem(s + step + p.ns, p.ns)},
+            device_id_type=MESH,
+        )
+
+    up_open, down_open = s + 1 < p.ns, s > 0
     for i in range(p.units):
-        unit = p.units * s + i
-        j = unit // p.parts - base
-        part = lax.rem(unit, p.parts)
+        j = place(s, 1) if i < 2 else place(s, 0)
+        part = i if i < 2 else s % 2
+        if i == 2:
+            for ds in range(1, p.ns):
+                level = lax.rem(s - ds + p.ns, p.ns)
+
+                @pl.when(expected(level))
+                def _():
+                    hand_on(level, place(peer_s, 0), place(s, 0)).wait_recv()
+
         q = got[pl.ds(part * per_part, per_part), j, 0].reshape(-1, HEAD_DIM)
         k = got[:, j, 1].reshape(-1, HEAD_DIM)
         v = got[:, j, 2].reshape(-1, HEAD_DIM)
@@ -304,82 +373,104 @@
         denominator = jnp.sum(weights, -1, keepdims=True)
         product = jnp.dot(weights.astype(jnp.bfloat16), v, preferred_element_type=jnp.float32)
         att[s, i] = (product / denominator).astype(jnp.bfloat16)
-        for ds in range(1, p.ns):
-            copy = pltpu.make_async_remote_copy(
-                src_ref=att.at[s, i],
-                dst_ref=att.at[s, i],
-                send_sem=s3.at[ds - 1, i],
-                recv_sem=r3.at[ds - 1, i],
-                device_id={"seq": lax.rem(s + ds, p.ns)},
-                device_id_type=MESH,
+        pl.when(up_open)(gather_hop(s, i, 1).start)
+        pl.when(down_open)(gather_hop(s, i, -1).start)
+
+    late[0].wait()
+    for distance in range(1, p.ns):
+        for i in range(p.units):
+
+            @pl.when(s - distance >= 0)
+            def _():
+                gather_hop(s - distance, i, 1).wait_recv()
+                pl.when(up_open)(gather_hop(s - distance, i, 1).start)
+
+            @pl.when(s + distance < p.ns)
+            def _():
+                gather_hop(s + distance, i, -1).wait_recv()
+                pl.when(down_open)(gather_hop(s + distance, i, -1).start)
+
+    def halving(c, b):
+        bit = (h >> b) & 1
+        source = term.at[c, :, :, 1 - bit] if b == 0 else landed[b - 1].at[c, :, 1 - bit]
+        return pltpu.make_async_remote_copy(
+            src_ref=source,
+            dst_ref=landed[b].at[c],
+            send_sem=s5.at[b, c],
+            recv_sem=r5.at[b, c],
+            device_id={"head": h + (1 - 2 * bit) * (1 << b)},
+            device_id_type=MESH,
+        )
+
+    per_seq = p.ns // p.parts
+    rows = []
+    for part in range(p.parts):
+        picks = [
+            att[2 * (g // 3) + part, 2] if g % 3 == 1 else att[2 * (g // 3) + g % 3 // 2, part]
+            for g in range(p.group)
+        ]
+        rows.append(jnp.concatenate(picks, axis=1))
+    for c in range(p.chunks):
+        cols = pl.ds(c * p.chunk, p.chunk)
+        for part in range(p.parts):
+            product = jnp.dot(rows[part], weight[:, cols], preferred_element_type=jnp.float32)
+            term[c, pl.ds(part * per_seq, per_seq)] = product.astype(jnp.bfloat16).reshape(
+                (per_seq,) + term.shape[2:]
             )
-            copy.start()
-            gather.append(copy)
-    late[0].wait()
-    for copy in gather:
-        copy.wait()
-
-    per_seq = p.ns // p.parts
-    for part in range(p.parts):
-        picks = [g * p.parts + part for g in range(p.group)]
-        rows = jnp.concatenate([att[u // p.units, u % p.units] for u in picks], axis=1)
-        product = jnp.dot(rows, weight[...], preferred_element_type=jnp.float32)
-        term[pl.ds(part * per_seq, per_seq)] = product.astype(jnp.bfloat16).reshape(
-            (per_seq,) + term.shape[1:]
-        )
-
-    current = term
-    for b in range(p.bits):
+        halving(c, 0).start()
+
+    def add_up(c, b):
         bit = (h >> b) & 1
-        peer = h + (1 - 2 * bit) * (1 << b)
-        half = p.nh >> (b + 1)
-        copy = pltpu.make_async_remote_copy(
-            src_ref=current.at[:, :, 1 - bit] if b == 0 else current.at[:, 1 - bit],
-            dst_ref=landed[b],
-            send_sem=s5.at[b],
-            recv_sem=r5.at[b],
-            device_id={"head": peer},
-            device_id_type=MESH,
-        )
-        copy.start()
-        copy.wait()
-        mine = current[:, :, bit] if b == 0 else current[:, bit]
-        total = mine.astype(jnp.float32) + landed[b][...].astype(jnp.float32)
-        landed[b][...] = total.astype(jnp.bfloat16)
-        current = landed[b]
-
-    owner = []
-    for ds in range(1, p.ns):
+        mine = term[c, :, :, bit] if b == 0 else landed[b - 1][c, :, bit]
+        total = mine.astype(jnp.float32) + landed[b][c].astype(jnp.float32)
+        landed[b][c] = total.astype(jnp.bfloat16)
+
+    for b in range(p.bits - 1):
+        for c in range(p.chunks):
+            halving(c, b).wait_recv()
+            add_up(c, b)
+            halving(c, b + 1).start()
+    summed = landed[p.bits - 1]
+
+    def to_owner(c, ds, slot):
         to_s = lax.rem(s + ds, p.ns)
-        copy = pltpu.make_async_remote_copy(
-            src_ref=current.at[to_s],
-            dst_ref=final.at[s],
-            send_sem=s6.at[ds - 1],
-            recv_sem=r6.at[ds - 1],
+        return pltpu.make_async_remote_copy(
+            src_ref=summed.at[c, to_s],
+            dst_ref=final.at[c, slot],
+            send_sem=s6.at[ds - 1, c],
+            recv_sem=r6.at[ds - 1, c],
             device_id={"seq": to_s},
             device_id_type=MESH,
         )
-        copy.start()
-        owner.append(copy)
-    final[s] = current[s]
+
+    for c in range(p.chunks):
+        halving(c, p.bits - 1).wait_recv()
+        add_up(c, p.bits - 1)
+        for ds in range(1, p.ns):
+            to_owner(c, ds, s).start()
+        final[c, s] = summed[c, s]
     for copy in late[1:]:
         copy.wait()
-    for copy in owner:
-        copy.wait()
 
     sums = jnp.zeros((p.tokens, 1), jnp.float32)
-    for j in range(p.ns):
-        cols = pl.ds(j * p.columns, p.columns)
-        value = res[:, cols].astype(jnp.float32) + gate_ref[:, cols] * final[j].astype(jnp.float32)
-        value = value.astype(jnp.bfloat16)
-        hidden_ref[:, cols] = value
-        sums = sums + jnp.sum(value.astype(jnp.float32), -1, keepdims=True)
+    for c in range(p.chunks):
+        for ds in range(1, p.ns):
+            to_owner(c, ds, lax.rem(s - ds + p.ns, p.ns)).wait_recv()
+        for j in range(p.ns):
+            cols = pl.ds(j * p.columns + c * p.chunk, p.chunk)
+            added = gate_ref[:, cols] * final[c, j].astype(jnp.float32)
+            value = (res[:, cols].astype(jnp.float32) + added).astype(jnp.bfloat16)
+            hidden_ref[:, cols] = value
+            sums = sums + jnp.sum(value.astype(jnp.float32), -1, keepdims=True)
     mean = sums / p.width
     center = hidden_ref[...].astype(jnp.float32) - mean
     spread = jnp.mean(center * center, -1, keepdims=True)
     normed = center * lax.rsqrt(spread + 1e-06) * (1.0 + scale_ref[...]) + shift_ref[...]
-    values = jnp.dot(
-        normed.astype(jnp.bfloat16), head_w[...], preferred_element_type=jnp.float32
+    values = lax.dot_general(
+        normed.astype(jnp.bfloat16),
+        head_w[...],
+        (((1,), (1,)), ((), ())),
+        preferred_element_type=jnp.float32,
     )
     values = (values + bias_ref[...]).astype(jnp.bfloat16)
     features = values.shape[-1]
@@ -429,6 +520,34 @@
         @pl.when(edge(index, 1))
         def _():
             hop(index).wait_send()
+
+    for k in range(2):
+        for index, (ds, dh) in enumerate(offsets):
+            to_s, copy = sending(index, k)
+            guarded(k, ds, s, to_s, copy.wait_send)
+    for ds in range(1, p.ns):
+        level = lax.rem(s - ds + p.ns, p.ns)
+
+        @pl.when(handed(level))
+        def _():
+            hand_on(level, place(s, 0), place(peer_s, 0)).wait_send()
+
+    for distance in range(p.ns):
+        for i in range(p.units):
+
+            @pl.when((s - distance >= 0) & up_open)
+            def _():
+                gather_hop(s - distance, i, 1).wait_send()
+
+            @pl.when((s + distance < p.ns) & down_open)
+            def _():
+                gather_hop(s + distance, i, -1).wait_send()
+
+    for c in range(p.chunks):
+        for b in range(p.bits):
+            halving(c, b).wait_send()
+        for ds in range(1, p.ns):
+            to_owner(c, ds, s).wait_send()
 
 
 def on_device(
@@ -456,12 +575,12 @@
     frames, height, breadth, inner = queries.shape
     t, width, patch_size = p.tokens, p.width, head_weight.shape[1]
     dma, bf16 = pltpu.SemaphoreType.DMA, jnp.bfloat16
-    tail = (t, p.columns)
+    tail = (t, p.chunk)
     lanes = -(-patch_size // 128) * 128
     any_spec = pl.BlockSpec(memory_space=pl.ANY)
     vmem = pl.BlockSpec(memory_space=pltpu.VMEM)
     landed = [
-        pltpu.VMEM((ns,) + ((nh >> 1,) if b == 0 and nh > 2 else ()) + tail, bf16)
+        pltpu.VMEM((p.chunks, ns) + ((nh >> 1,) if b == 0 and nh > 2 else ()) + tail, bf16)
         for b in range(p.bits)
     ]
     hidden, near = pl.pallas_call(
@@ -474,31 +593,33 @@
         out_specs=(vmem, vmem),
         scratch_shapes=[
             pltpu.VMEM((3, t, inner), bf16),
-            pltpu.VMEM((p.slots, p.span, 3, t, HEAD_DIM), bf16),
+            pltpu.VMEM((p.slots, 2, 3, t, HEAD_DIM), bf16),
             pltpu.VMEM((ns, p.units, p.slots // p.parts * t, HEAD_DIM), bf16),
             pltpu.VMEM(out_weight.shape, bf16),
             pltpu.VMEM((t, width), bf16),
-            pltpu.VMEM(head_weight.shape, bf16),
-            pltpu.VMEM((ns, nh >> 1, 2) + tail, bf16),
+            pltpu.VMEM(head_weight.shape[::-1], bf16),
+            pltpu.VMEM((p.chunks, ns, nh >> 1, 2) + tail, bf16),
             *landed,
-            pltpu.VMEM((ns,) + tail, bf16),
+            pltpu.VMEM((p.chunks, ns) + tail, bf16),
             pltpu.VMEM((t, lanes), bf16),
             pltpu.VMEM((5, t, lanes), bf16),
             dma((6,)),
-            dma((p.span,)),
-            dma((p.slots - 1, p.span)),
-            dma((p.slots - 1, p.span)),
-            dma((ns - 1, p.units)),
-            dma((ns - 1, p.units)),
-            dma((p.bits,)),
-            dma((p.bits,)),
-            dma((ns - 1,)),
-            dma((ns - 1,)),
+            dma((2,)),
+            dma((p.slots - 1, 2)),
+            dma((p.slots - 1, 2)),
+            dma((ns,)),
+            dma((ns,)),
+            dma((2, ns, p.units)),
+            dma((ns, p.units)),
+            dma((p.bits, p.chunks)),
+            dma((p.bits, p.chunks)),
+            dma((ns - 1, p.chunks)),
+            dma((ns - 1, p.chunks)),
             dma((5,)),
             dma((5,)),
         ],
         compiler_params=pltpu.CompilerParams(
-            collective_id=0, has_side_effects=True, vmem_limit_bytes=40 * 1024 * 1024
+            collective_id=0, has_side_effects=True, vmem_limit_bytes=60 * 1024 * 1024
         ),
     )(
         queries.reshape(t, inner),
@@ -506,7 +627,7 @@
         attn_values.reshape(t, inner),
         residual.reshape(t, width),
         out_weight,
-        head_weight,
+        head_weight.T,
         out_gate.reshape(1, -1),
         head_shift.reshape(1, -1),
         head_scale.reshape(1, -1),

time: 74.5 us -> 60.7 us (0.81)
  Pallas kernels: 66.4 us -> 55.1 us
  local copies, waits for them, and re-layouts: 5.84 us -> 3.45 us
    pallas_call x1, Pallas kernels: 66.4 us -> 55.1 us  [on_device(): pl.pallas_call(functools.partial(block_kernel, p), out_shape=(jax.ShapeDt...]
    unnamed x26 -> x9, local copies, waits for them, and re-layouts: 4.9 us -> 1.71 us
    reshape x2, local copies, waits for them, and re-layouts: 0.29 us -> 1.1 us  [on_device(): video = near.reshape(2, 3, frames, height, breadth, 2, 2, channels)]
where the time goes in v2:
time: 60.7 us; the launch traced here: 60.4 us
  Pallas kernels  55.1 us (91%)
  local copies, waits for them, and re-layouts  3.45 us (6%)
  other arithmetic  0.84 us (1%)
  between operations  0.75 us (1%)
    pallas_call x1, Pallas kernels, on_device(): pl.pallas_call(functools.partial(block_kernel, p), out_shape=(jax.ShapeDt...  55.1 us
    unnamed x9, local copies, waits for them, and re-layouts  1.71 us

profile of v2, /device:TPU:0, one launch (start us, length us, event | category | flops | bytes accessed | tf_op | source)
XLA Modules:
  0.0 60.4 jit_solution(7078370284887533994)
XLA Ops:
  0.6 0.0 copy-start
  0.6 1.0 %copy-done = bf16[3,3,3,16,384]{4,3,2,1,0:T(8,128)(2,1)S(1)} copy-done((bf16[3,3,3,16,384]{4,3,2,1,0:T(8,128)(2,1)S(1)}, bf16[3,3,3,16,384]{4,3,2,1,0:T(8,128)(2,1)}, u32[]{:S(2)}) %copy-start) | copy-done | bytes 331800
  1.6 55.1 %shard_map.140 = (bf16[32,5120]{1,0:T(8,128)(2,1)}, bf16[2,3,32,64]{3,2,1,0:T(8,128)(2,1)}) custom-call(bf16[32,3072]{1,0:T(8,128)(2,1)} %bitcast.34, bf16[32,3072]{1,0:T(8,128)(2,1)} %bitcast.35, bf16[32,3072]{1,0:T(8,128)(2,1)} %bitcast.36, bf16[32,5120]{1,0:T(8,128)(2,1)} %bitcast.32, bf16[768,1280]{1,0:T(8,128)(2,1)} %w_hbm.1, ...), custom_call_target="tpu_custom_call" | custom-call | tf_op jit(solution)/shard_map/pallas_call | solution.py:586
  56.7 0.0 copy-start.2
  56.7 0.9 %reshape.67 = bf16[2,3,2,1,16,2,2,16]{7,6,5,4,2,1,0,3:T(2,128)(2,1)S(1)} reshape(bf16[2,3,32,64]{3,2,1,0:T(8,128)(2,1)} %get-tuple-element.5) | data formatting | bytes 49152 | tf_op jit(solution)/shard_map/reshape | solution.py:637
  57.6 0.2 copy.19
  57.8 0.0 copy-start.3
  57.8 0.2 fusion.3
  58.0 0.0 copy-start.1
  58.1 0.1 pad_slice_fusion.6
  58.2 0.3 concatenate.7
  58.6 0.0 copy-done.2
  58.6 0.3 multiply_reduce_fusion
  58.9 0.0 copy-done.3
  58.9 0.8 %multiply_convert_fusion = bf16[128,384]{1,0:T(8,128)(2,1)} fusion(f32[128,384]{1,0:T(8,128)S(1)} %get-tuple-element.40, f32[384]{0:T(512)S(1)} %copy-done.3, f32[128]{0:T(128)S(1)} %add_rsqrt_fusion), kind=kLoop, calls=%fused_computation.8 | loop fusion | flops 344064 | bytes 296960 | tf_op jit(solution)/shard_map/convert_element_type | solution.py:72
  59.7 0.0 copy-done.1
  59.7 0.7 %copy.21 = bf16[2,1,16,5120]{3,2,1,0:T(8,128)(2,1)} copy(bf16[2,1,16,5120]{3,2,1,0:T(8,128)(2,1)S(1)} %bitcast.33) | data formatting | bytes 655360
  (3 shorter events, 0.1 us)
Async XLA Ops:
  0.6 1.0 %copy-start = (bf16[3,3,3,16,384]{4,3,2,1,0:T(8,128)(2,1)S(1)}, bf16[3,3,3,16,384]{4,3,2,1,0:T(8,128)(2,1)}, u32[]{:S(2)}) copy-start(bf16[3,3,3,16,384]{4,3,2,1,0:T(8,128)(2,1)} %param.23) | copy-start | bytes 995332
  56.7 1.9 %copy-start.2 = (f32[384]{0:T(512)S(1)}, f32[384]{0:T(512)}, u32[]{:S(2)}) copy-start(f32[384]{0:T(512)} %param.24) | copy-start | bytes 4612
  57.8 1.1 %copy-start.3 = (f32[384]{0:T(512)S(1)}, f32[384]{0:T(512)}, u32[]{:S(2)}) copy-start(f32[384]{0:T(512)} %param.25) | copy-start | bytes 4612
  58.0 1.7 %copy-start.1 = (bf16[32,5120]{1,0:T(8,128)(2,1)S(1)}, bf16[32,5120]{1,0:T(8,128)(2,1)}, u32[]{:S(2)}) copy-start(bf16[32,5120]{1,0:T(8,128)(2,1)} %get-tuple-element.4) | copy-start | bytes 983044

commit v3 on v2

--- a/solution.py
+++ b/solution.py
@@ -223,7 +223,6 @@
     (local_sem, own_sem, s1, r1, sf, rf, s3, r3, s5, r5, s6, r6, s7, r7) = rest[p.bits + 3 :]
     s = lax.axis_index("seq")
     h = lax.axis_index("head")
-    here = s * p.nh + h
 
     loads = [
         pltpu.make_async_copy(q_hbm, qkv.at[0], local_sem.at[0]),
@@ -263,10 +262,10 @@
         down = (source // 2 > target // 2) & (target % 2 == 0)
         return jnp.logical_not(up | down)
 
-    def first_hop(index, k, to_s, to_h, slot, j):
+    def first_hop(index, k, to_s, to_h, from_s, from_h, j):
         return pltpu.make_async_remote_copy(
             src_ref=piece(to_s, to_h, j),
-            dst_ref=got.at[slot, j],
+            dst_ref=got.at[from_h % 2, from_s, from_h // 2, j],
             send_sem=s1.at[index, k],
             recv_sem=r1.at[index, k],
             device_id={"seq": to_s, "head": to_h},
@@ -276,12 +275,12 @@
     def sending(index, k):
         ds, dh = offsets[index]
         to_s, to_h = lax.rem(s + ds, p.ns), lax.rem(h + dh, p.nh)
-        return to_s, first_hop(index, k, to_s, to_h, here, place(to_s, k))
+        return to_s, first_hop(index, k, to_s, to_h, s, h, place(to_s, k))
 
     def arriving(index, k):
         ds, dh = offsets[index]
         from_s, from_h = lax.rem(s - ds + p.ns, p.ns), lax.rem(h - dh + p.nh, p.nh)
-        return from_s, first_hop(index, k, s, h, from_s * p.nh + from_h, place(s, k))
+        return from_s, first_hop(index, k, s, h, from_s, from_h, place(s, k))
 
     def guarded(k, ds, source, target, act):
         if k == 0 and ds:
@@ -294,7 +293,8 @@
             to_s, copy = sending(index, k)
             guarded(k, ds, s, to_s, copy.start)
     own = [
-        pltpu.make_async_copy(piece(s, h, j), got.at[here, j], own_sem.at[j]) for j in range(2)
+        pltpu.make_async_copy(piece(s, h, j), got.at[h % 2, s, h // 2, j], own_sem.at[j])
+        for j in range(2)
     ]
     for copy in own:
         copy.start()
@@ -307,10 +307,9 @@
     peer_s = s + 1 - 2 * (s % 2)
 
     def hand_on(level, j_from, j_to):
-        rows = pl.ds(level * p.nh, p.nh)
         return pltpu.make_async_remote_copy(
-            src_ref=got.at[rows, j_from, pl.ds(1, 2)],
-            dst_ref=got.at[rows, j_to, pl.ds(1, 2)],
+            src_ref=got.at[:, level, :, j_from],
+            dst_ref=got.at[:, level, :, j_to],
             send_sem=sf.at[level],
             recv_sem=rf.at[level],
             device_id={"seq": peer_s},
@@ -335,10 +334,6 @@
             def _():
                 hand_on(level, place(s, 0), place(peer_s, 0)).start()
 
-    for index in range(len(offsets)):
-        arriving(index, 1)[1].wait_recv()
-
-    per_part = p.slots // p.parts
 
     def gather_hop(source, i, step):
         return pltpu.make_async_remote_copy(
@@ -351,7 +346,8 @@
         )
 
     up_open, down_open = s + 1 < p.ns, s > 0
-    for i in range(p.units):
+    order = (2, 0, 1)
+    for i in order:
         j = place(s, 1) if i < 2 else place(s, 0)
         part = i if i < 2 else s % 2
         if i == 2:
@@ -362,9 +358,12 @@
                 def _():
                     hand_on(level, place(peer_s, 0), place(s, 0)).wait_recv()
 
-        q = got[pl.ds(part * per_part, per_part), j, 0].reshape(-1, HEAD_DIM)
-        k = got[:, j, 1].reshape(-1, HEAD_DIM)
-        v = got[:, j, 2].reshape(-1, HEAD_DIM)
+        if i == 0:
+            for index in range(len(offsets)):
+                arriving(index, 1)[1].wait_recv()
+        q = got[part, :, :, j, 0].reshape(-1, HEAD_DIM)
+        k = got[:, :, :, j, 1].reshape(-1, HEAD_DIM)
+        v = got[:, :, :, j, 2].reshape(-1, HEAD_DIM)
         scores = lax.dot_general(
             q, k, (((1,), (1,)), ((), ())), preferred_element_type=jnp.float32
         )
@@ -377,22 +376,29 @@
         pl.when(down_open)(gather_hop(s, i, -1).start)
 
     late[0].wait()
-    for distance in range(1, p.ns):
-        for i in range(p.units):
-
-            @pl.when(s - distance >= 0)
-            def _():
-                gather_hop(s - distance, i, 1).wait_recv()
-                pl.when(up_open)(gather_hop(s - distance, i, 1).start)
-
-            @pl.when(s + distance < p.ns)
-            def _():
-                gather_hop(s + distance, i, -1).wait_recv()
-                pl.when(down_open)(gather_hop(s + distance, i, -1).start)
+
+    def relay(i, distance):
+        @pl.when(s - distance >= 0)
+        def _():
+            gather_hop(s - distance, i, 1).wait_recv()
+            pl.when(up_open)(gather_hop(s - distance, i, 1).start)
+
+        @pl.when(s + distance < p.ns)
+        def _():
+            gather_hop(s + distance, i, -1).wait_recv()
+            pl.when(down_open)(gather_hop(s + distance, i, -1).start)
+
+    waves = sorted(
+        (position + distance, position, i, distance)
+        for position, i in enumerate(order)
+        for distance in range(1, p.ns)
+    )
+    for _, _, i, distance in waves[:-1]:
+        relay(i, distance)
 
     def halving(c, b):
         bit = (h >> b) & 1
-        source = term.at[c, :, :, 1 - bit] if b == 0 else landed[b - 1].at[c, :, 1 - bit]
+        source = term.at[c, 1 - bit] if b == 0 else landed[b - 1].at[c, :, 1 - bit]
         return pltpu.make_async_remote_copy(
             src_ref=source,
             dst_ref=landed[b].at[c],
@@ -402,34 +408,33 @@
             device_id_type=MESH,
         )
 
-    per_seq = p.ns // p.parts
-    rows = []
+    def add_up(c, b):
+        bit = (h >> b) & 1
+        mine = term[c, bit] if b == 0 else landed[b - 1][c, :, bit]
+        total = mine.astype(jnp.float32) + landed[b][c].astype(jnp.float32)
+        landed[b][c] = total.astype(jnp.bfloat16)
+
     for part in range(p.parts):
+        if part == p.parts - 1:
+            relay(*waves[-1][2:])
         picks = [
             att[2 * (g // 3) + part, 2] if g % 3 == 1 else att[2 * (g // 3) + g % 3 // 2, part]
             for g in range(p.group)
         ]
-        rows.append(jnp.concatenate(picks, axis=1))
-    for c in range(p.chunks):
-        cols = pl.ds(c * p.chunk, p.chunk)
-        for part in range(p.parts):
-            product = jnp.dot(rows[part], weight[:, cols], preferred_element_type=jnp.float32)
-            term[c, pl.ds(part * per_seq, per_seq)] = product.astype(jnp.bfloat16).reshape(
-                (per_seq,) + term.shape[2:]
-            )
-        halving(c, 0).start()
-
-    def add_up(c, b):
-        bit = (h >> b) & 1
-        mine = term[c, :, :, bit] if b == 0 else landed[b - 1][c, :, bit]
-        total = mine.astype(jnp.float32) + landed[b][c].astype(jnp.float32)
-        landed[b][c] = total.astype(jnp.bfloat16)
-
-    for b in range(p.bits - 1):
+        rows = jnp.concatenate(picks, axis=1)
         for c in range(p.chunks):
-            halving(c, b).wait_recv()
-            add_up(c, b)
-            halving(c, b + 1).start()
+            cols = pl.ds(c * p.chunk, p.chunk)
+            product = jnp.dot(rows, weight[:, cols], preferred_element_type=jnp.float32)
+            term[c, part] = product.astype(jnp.bfloat16).reshape(term.shape[2:])
+            pl.when(h % 2 != part)(halving(c, 0).start)
+
+        @pl.when(h % 2 == part)
+        def _():
+            for c in range(p.chunks):
+                halving(c, 0).wait_recv()
+                add_up(c, 0)
+                halving(c, 1).start()
+
     summed = landed[p.bits - 1]
 
     def to_owner(c, ds, slot):
@@ -593,12 +598,12 @@
         out_specs=(vmem, vmem),
         scratch_shapes=[
             pltpu.VMEM((3, t, inner), bf16),
-            pltpu.VMEM((p.slots, 2, 3, t, HEAD_DIM), bf16),
+            pltpu.VMEM((2, ns, nh >> 1, 2, 3, t, HEAD_DIM), bf16),
             pltpu.VMEM((ns, p.units, p.slots // p.parts * t, HEAD_DIM), bf16),
             pltpu.VMEM(out_weight.shape, bf16),
             pltpu.VMEM((t, width), bf16),
             pltpu.VMEM(head_weight.shape[::-1], bf16),
-            pltpu.VMEM((p.chunks, ns, nh >> 1, 2) + tail, bf16),
+            pltpu.VMEM((p.chunks, 2, ns, nh >> 1) + tail, bf16),
             *landed,
             pltpu.VMEM((p.chunks, ns) + tail, bf16),
             pltpu.VMEM((t, lanes), bf16),

time: 60.7 us -> 62.7 us (1.033)
  Pallas kernels: 55.1 us -> 57 us
    pallas_call x1, Pallas kernels: 55.1 us -> 57 us  [on_device(): pl.pallas_call(functools.partial(block_kernel, p), out_shape=(jax.ShapeDt...]
where the time goes in v3:
time: 62.7 us; the launch traced here: 62.4 us
  Pallas kernels  57 us (91%)
  local copies, waits for them, and re-layouts  3.45 us (6%)
  other arithmetic  0.84 us (1%)
  between operations  0.75 us (1%)
    pallas_call x1, Pallas kernels, on_device(): pl.pallas_call(functools.partial(block_kernel, p), out_shape=(jax.ShapeDt...  57 us
    unnamed x9, local copies, waits for them, and re-layouts  1.71 us

profile of v3, /device:TPU:0, one launch (start us, length us, event | category | flops | bytes accessed | tf_op | source)
XLA Modules:
  0.0 62.4 jit_solution(18349339365859663473)
XLA Ops:
  0.6 0.0 copy-start
  0.6 1.0 %copy-done = bf16[3,3,3,16,384]{4,3,2,1,0:T(8,128)(2,1)S(1)} copy-done((bf16[3,3,3,16,384]{4,3,2,1,0:T(8,128)(2,1)S(1)}, bf16[3,3,3,16,384]{4,3,2,1,0:T(8,128)(2,1)}, u32[]{:S(2)}) %copy-start) | copy-done | bytes 331800
  1.6 57.0 %shard_map.140 = (bf16[32,5120]{1,0:T(8,128)(2,1)}, bf16[2,3,32,64]{3,2,1,0:T(8,128)(2,1)}) custom-call(bf16[32,3072]{1,0:T(8,128)(2,1)} %bitcast.34, bf16[32,3072]{1,0:T(8,128)(2,1)} %bitcast.35, bf16[32,3072]{1,0:T(8,128)(2,1)} %bitcast.36, bf16[32,5120]{1,0:T(8,128)(2,1)} %bitcast.32, bf16[768,1280]{1,0:T(8,128)(2,1)} %w_hbm.1, ...), custom_call_target="tpu_custom_call" | custom-call | tf_op jit(solution)/shard_map/pallas_call | solution.py:591
  58.7 0.0 copy-start.2
  58.7 0.9 %reshape.67 = bf16[2,3,2,1,16,2,2,16]{7,6,5,4,2,1,0,3:T(2,128)(2,1)S(1)} reshape(bf16[2,3,32,64]{3,2,1,0:T(8,128)(2,1)} %get-tuple-element.5) | data formatting | bytes 49152 | tf_op jit(solution)/shard_map/reshape | solution.py:642
  59.6 0.2 copy.19
  59.8 0.0 copy-start.3
  59.8 0.2 fusion.3
  60.0 0.0 copy-start.1
  60.1 0.1 pad_slice_fusion.6
  60.2 0.3 concatenate.7
  60.5 0.0 copy-done.2
  60.6 0.3 multiply_reduce_fusion
  60.9 0.0 copy-done.3
  60.9 0.8 %multiply_convert_fusion = bf16[128,384]{1,0:T(8,128)(2,1)} fusion(f32[128,384]{1,0:T(8,128)S(1)} %get-tuple-element.40, f32[384]{0:T(512)S(1)} %copy-done.3, f32[128]{0:T(128)S(1)} %add_rsqrt_fusion), kind=kLoop, calls=%fused_computation.8 | loop fusion | flops 344064 | bytes 296960 | tf_op jit(solution)/shard_map/convert_element_type | solution.py:72
  61.7 0.0 copy-done.1
  61.7 0.7 %copy.21 = bf16[2,1,16,5120]{3,2,1,0:T(8,128)(2,1)} copy(bf16[2,1,16,5120]{3,2,1,0:T(8,128)(2,1)S(1)} %bitcast.33) | data formatting | bytes 655360
  (3 shorter events, 0.1 us)
Async XLA Ops:
  0.6 1.0 %copy-start = (bf16[3,3,3,16,384]{4,3,2,1,0:T(8,128)(2,1)S(1)}, bf16[3,3,3,16,384]{4,3,2,1,0:T(8,128)(2,1)}, u32[]{:S(2)}) copy-start(bf16[3,3,3,16,384]{4,3,2,1,0:T(8,128)(2,1)} %param.23) | copy-start | bytes 995332
  58.7 1.9 %copy-start.2 = (f32[384]{0:T(512)S(1)}, f32[384]{0:T(512)}, u32[]{:S(2)}) copy-start(f32[384]{0:T(512)} %param.24) | copy-start | bytes 4612
  59.8 1.1 %copy-start.3 = (f32[384]{0:T(512)S(1)}, f32[384]{0:T(512)}, u32[]{:S(2)}) copy-start(f32[384]{0:T(512)} %param.25) | copy-start | bytes 4612
  60.0 1.7 %copy-start.1 = (bf16[32,5120]{1,0:T(8,128)(2,1)S(1)}, bf16[32,5120]{1,0:T(8,128)(2,1)}, u32[]{:S(2)}) copy-start(bf16[32,5120]{1,0:T(8,128)(2,1)} %get-tuple-element.4) | copy-start | bytes 983044
